TPU v7x, 32 devices: a whole 2x2x4 slice. The times are simulated.
32 devices in a mesh: groups: 2 (over y), gx: 4 (over z), gy: 4 (over x, core).
Axes of the slice: x: 2, y: 2, z: 4, core: 2. Of those that a mesh axis runs over, the one named last changes fastest.
Arguments:
- thermal_deviation: float32 [32, 256, 512], P('groups', 'gy', 'gx'), parts along dimension 0, may hold values from -6 to 6
- brine_content: float32 [32, 256, 512], P('groups', 'gy', 'gx'), parts along dimension 0, may hold values from 0.2 to 2.4
- current_components: float32 [4, 16, 256, 512], P('groups', None, 'gy', 'gx'), parts along dimension 0, may hold values from -4 to 4
- sea_indicator: int32 [256, 512], P('gy', 'gx'), may hold values from 0 to 1, as said below
- flooded_layer_number: int32 [256, 512], P('gy', 'gx'), may hold values from 1 to 16
- footprint_square_metres: float32 [256, 512], P('gy', 'gx'), may hold values from 0.5 to 5
- rainfall_input: float32 [256, 512], P('gy', 'gx'), may hold values from -2 to 3.5
- seam_partner_index: int32 [512], P('gx'), may hold values from 0 to 511, as said below
Outputs:
- temperature_next: float32 [32, 256, 512], P('groups', 'gy', 'gx'), parts along dimension 0
- salinity_next: float32 [32, 256, 512], P('groups', 'gy', 'gx'), parts along dimension 0
There are 2 independent parts, one for each index of `groups`. A program takes and returns all parts, laid end to end along the dimension named above; an argument that names none is the same for every part. Nothing has to cross between parts.
Inputs may be any that keep to these rules, and one draw needn't show every extreme that they name: `sea_indicator`: at least one column is ocean. seam_partner_index[x] = (s - x) mod 512 for one s of each draw with s mod 128 = 127; the map is its own inverse and has no fixed point.
All inputs are finite; a program needn't handle non-finite values.
Results may differ from a plain program's by a relative error of at most 0.00002.
Values sent between devices are 32-bit elements; how exact they have to be, the bound alone decides.
A program may use at most 64 MiB of HBM per device.

v0:
```python
import jax
import jax.numpy as jnp
from jax import lax
from jax.sharding import PartitionSpec as P

time_step = 0.25
diffusivity = 0.5
vertical_mixing = 0.3
top_thickness = 0.5


def with_halo(cells, sides, width, closed):
    for axis, dim in sides:
        count = lax.axis_size(axis)
        ends = count if closed else count - 1
        head = lax.slice_in_dim(cells, 0, width, axis=dim)
        tail = lax.slice_in_dim(cells, cells.shape[dim] - width, cells.shape[dim], axis=dim)
        cells = jnp.concatenate(
            [
                lax.ppermute(tail, axis, [(i, (i + 1) % count) for i in range(ends)]),
                cells,
                lax.ppermute(head, axis, [((i + 1) % count, i) for i in range(ends)]),
            ],
            axis=dim,
        )
    return cells


def face_flux(near_cells, far_cells, face_speed, near_wet, far_wet):
    upwind = jnp.maximum(face_speed, 0.0) * near_cells + jnp.minimum(face_speed, 0.0) * far_cells
    return near_wet * far_wet * (upwind - diffusivity * (far_cells - near_cells))


def wet_from(depth_plane, layer_stack_number):
    level_index = jnp.arange(layer_stack_number, dtype=jnp.float32)
    return (level_index[:, None, None] < depth_plane[None]).astype(jnp.float32)


def split_tracer(block_planes, layer_stack_number):
    return block_planes[: 2 * layer_stack_number].reshape(
        (2, layer_stack_number) + block_planes.shape[1:]
    )


def shards(
    thermal_deviation,
    brine_content,
    current_components,
    sea_indicator,
    flooded_layer_number,
    footprint_square_metres,
    rainfall_input,
    seam_partner_index,
):
    layer_stack_number, parallel_total_number, meridian_total_number = thermal_deviation.shape
    stacked_layer_number = (sea_indicator * flooded_layer_number).astype(jnp.float32)
    wet_area = footprint_square_metres * sea_indicator.astype(jnp.float32)
    surface = brine_content[0]
    total_area, total_fresh, salt_fresh, salt_only = lax.psum(
        (
            jnp.sum(wet_area),
            jnp.sum(wet_area * rainfall_input),
            jnp.sum(wet_area * surface * rainfall_input),
            jnp.sum(wet_area * surface),
        ),
        ("gx", "gy"),
    )
    mean_fresh = total_fresh / total_area
    balanced = rainfall_input - mean_fresh
    total_salt = salt_fresh - mean_fresh * salt_only
    virtual = -surface * balanced + total_salt / total_area
    top_row = jnp.concatenate(
        [
            thermal_deviation[:, -1, :],
            brine_content[:, -1, :],
            current_components[1][:, -1, :],
            stacked_layer_number[-1:, :],
        ],
        axis=0,
    )
    gathered = lax.all_gather(top_row, "gx", axis=1, tiled=True)
    partner_row = jnp.take(gathered, seam_partner_index, axis=1)
    partner_fields = jnp.concatenate(
        [partner_row[: 2 * layer_stack_number], partner_row[3 * layer_stack_number :]], axis=0
    )
    partner_speed = partner_row[2 * layer_stack_number : 3 * layer_stack_number]
    is_top = lax.axis_index("gy") == lax.axis_size("gy") - 1
    planes = jnp.concatenate(
        [
            thermal_deviation,
            brine_content,
            current_components[0],
            current_components[1],
            stacked_layer_number[None],
        ],
        axis=0,
    )
    zonal_padded = with_halo(planes, (("gx", 2),), 1, True)
    meridional_padded = with_halo(planes, (("gy", 1),), 1, False)
    zonal_tracer = split_tracer(zonal_padded, layer_stack_number)
    zonal_wet = wet_from(zonal_padded[4 * layer_stack_number], layer_stack_number)
    zonal_near_speed = zonal_padded[2 * layer_stack_number : 3 * layer_stack_number][..., :-1]
    halo_top = jnp.concatenate(
        [
            meridional_padded[: 2 * layer_stack_number, -1, :],
            meridional_padded[4 * layer_stack_number :, -1, :],
        ],
        axis=0,
    )
    above_fields = jnp.where(is_top, partner_fields, halo_top)
    upper_tracer_cells = jnp.concatenate(
        [
            meridional_padded[: 2 * layer_stack_number, 1:-1, :],
            above_fields[: 2 * layer_stack_number, None, :],
        ],
        axis=1,
    )
    upper_depth = jnp.concatenate(
        [
            meridional_padded[4 * layer_stack_number, 1:-1, :],
            above_fields[2 * layer_stack_number][None, :],
        ],
        axis=0,
    )
    lower_cells = meridional_padded[:, :-1, :]
    lower_tracer = split_tracer(lower_cells, layer_stack_number)
    lower_wet = wet_from(lower_cells[4 * layer_stack_number], layer_stack_number)
    upper_tracer = split_tracer(upper_tracer_cells, layer_stack_number)
    upper_wet = wet_from(upper_depth, layer_stack_number)
    north_speed = lower_cells[3 * layer_stack_number : 4 * layer_stack_number]
    carried_quantity = jnp.stack([thermal_deviation, brine_content])
    wet_cells = wet_from(stacked_layer_number, layer_stack_number)
    zonal_flux = face_flux(
        zonal_tracer[..., :-1],
        zonal_tracer[..., 1:],
        zonal_near_speed,
        zonal_wet[..., :-1],
        zonal_wet[..., 1:],
    )
    fold_speed = 0.5 * (north_speed[:, -1, :] - partner_speed)
    last_speed = jnp.where(is_top, fold_speed, north_speed[:, -1, :])
    north_speed = jnp.concatenate([north_speed[:, :-1, :], last_speed[:, None, :]], axis=1)
    meridional_flux = face_flux(lower_tracer, upper_tracer, north_speed, lower_wet, upper_wet)
    vertical = (
        wet_cells[:-1]
        * wet_cells[1:]
        * vertical_mixing
        * (carried_quantity[:, :-1] - carried_quantity[:, 1:])
    )
    zero_layer = jnp.zeros_like(vertical[:, :1])
    from_above = jnp.concatenate([zero_layer, vertical], axis=1)
    to_below = jnp.concatenate([vertical, zero_layer], axis=1)
    tendency = time_step / footprint_square_metres * (
        zonal_flux[..., :-1]
        - zonal_flux[..., 1:]
        + meridional_flux[:, :, :-1]
        - meridional_flux[:, :, 1:]
    ) + time_step * (from_above - to_below)
    updated = carried_quantity + wet_cells * tendency
    surface_next = updated[1, 0] + time_step / top_thickness * virtual * wet_cells[0]
    salinity_next = jnp.concatenate([surface_next[None], updated[1, 1:]], axis=0)
    return (updated[0], salinity_next)


def solution(mesh):
    in_specs = (
        P("groups", "gy", "gx"),
        P("groups", "gy", "gx"),
        P("groups", None, "gy", "gx"),
        P("gy", "gx"),
        P("gy", "gx"),
        P("gy", "gx"),
        P("gy", "gx"),
        P("gx"),
    )
    out_specs = (P("groups", "gy", "gx"), P("groups", "gy", "gx"))
    return jax.shard_map(shards, mesh=mesh, in_specs=in_specs, out_specs=out_specs, check_vma=False)
```

profile of v0, /device:TPU:0, one launch (start us, length us, event | category | flops | bytes accessed | tf_op | source)
XLA Modules:
  0.0 111.4 jit_solution(16813490816440808588)
XLA Ops:
  0.6 2.3 %constant_dynamic-update-slice_fusion.2 = (f32[65,64,128]{2,0,1:T(8,128)S(1)}, f32[16,64,128]{2,0,1:T(8,128)}) fusion(f32[16,64,128]{2,1,0:T(8,128)} %param.8), kind=kLoop, calls=%fused_computation.82 | loop fusion | bytes 1572864
  3.1 1.1 %constant_dynamic-update-slice_fusion.1 = (f32[65,64,128]{2,0,1:T(8,128)S(1)}, f32[16,64,128]{2,0,1:T(8,128)}) fusion(f32[65,64,128]{2,0,1:T(8,128)S(1)} %get-tuple-element.22, f32[16,64,128]{2,1,0:T(8,128)S(1)} %copy-done.2), kind=kLoop, calls=%fused_computation.81 | loop fusion | bytes 1572864
  5.0 2.9 %fusion.24 = (f32[65,64,1]{2,0,1:T(8,128)}, f32[65,64,1]{2,0,1:T(8,128)}) fusion(f32[65,64,128]{2,0,1:T(8,128)S(1)} %dynamic-update-slice.4), kind=kLoop, calls=%fused_computation.87 | loop fusion | bytes 66560 | tf_op jit(solution)/shard_map/slice | solution.py:17
  7.9 3.1 %copy.160 = f32[65,64,1]{0,1,2:T(8,128)} copy(f32[65,64,1]{2,0,1:T(8,128)} %get-tuple-element.14) | data formatting | bytes 33280 | tf_op jit(solution)/shard_map/slice | solution.py:17
  11.0 3.1 %collective-permute-start = (f32[65,64,1]{0,1,2:T(8,128)}, f32[65,64,1]{0,1,2:T(8,128)}, u32[]{:S(2)}, u32[]{:S(2)}) collective-permute-start(f32[65,64,1]{0,1,2:T(8,128)} %copy.160), channel_id=1, source_target_pairs={{0,4},{4,8},{8,12},{12,0},{1,5},{5,9},{9,13},{13,1},{2,6},{6,10},{... | collective-permute-start | bytes 49928 | tf_op jit(solution)/shard_map/ppermute | solution.py:20
  14.0 3.1 %copy.161 = f32[65,64,1]{0,1,2:T(8,128)} copy(f32[65,64,1]{2,0,1:T(8,128)} %get-tuple-element.15) | data formatting | bytes 33280 | tf_op jit(solution)/shard_map/slice | solution.py:16
  17.1 2.1 %collective-permute-start.1 = (f32[65,64,1]{0,1,2:T(8,128)}, f32[65,64,1]{0,1,2:T(8,128)}, u32[]{:S(2)}, u32[]{:S(2)}) collective-permute-start(f32[65,64,1]{0,1,2:T(8,128)} %copy.161), channel_id=1, source_target_pairs={{4,0},{8,4},{12,8},{0,12},{5,1},{9,5},{13,9},{1,13},{6,2},{10,6},{... | collective-permute-start | bytes 49928 | tf_op jit(solution)/shard_map/ppermute | solution.py:22
  19.2 0.6 fusion.25
  19.8 1.3 %collective-permute-start.2 = (f32[65,1,128]{2,0,1:T(8,128)}, f32[65,1,128]{2,0,1:T(8,128)}, u32[]{:S(2)}, u32[]{:S(2)}) collective-permute-start(f32[65,1,128]{2,0,1:T(8,128)} %get-tuple-element.17), channel_id=1, source_target_pairs={{1,0},{2,1},{3,2},{5,4},{6,5},{7,6},{9,8},{10,9},{11,10},{13,12},{... | collective-permute-start | bytes 99848 | tf_op jit(solution)/shard_map/ppermute | solution.py:22
  21.1 3.6 %collective-permute-start.3 = (f32[65,1,128]{2,0,1:T(8,128)}, f32[65,1,128]{2,0,1:T(8,128)}, u32[]{:S(2)}, u32[]{:S(2)}) collective-permute-start(f32[65,1,128]{2,0,1:T(8,128)} %get-tuple-element.16), channel_id=1, source_target_pairs={{0,1},{1,2},{2,3},{4,5},{5,6},{6,7},{8,9},{9,10},{10,11},{12,13},{... | collective-permute-start | bytes 99848 | tf_op jit(solution)/shard_map/ppermute | solution.py:20
  24.7 1.3 %copy.203 = f32[1,16,64,128]{3,1,2,0:T(8,128)S(1)} copy(f32[1,16,64,128]{3,2,1,0:T(8,128)} %copy-done.5) | data formatting | bytes 1048576
  26.1 0.7 compare_select_fusion
  26.8 0.5 compare_and_fusion
  27.3 1.1 pad_maximum_fusion.6
  28.4 0.8 fusion.11
  29.2 0.7 slice_bitcast_fusion.7
  29.9 0.7 slice_bitcast_fusion.5
  30.6 13.3 %all_gather.3 = f32[49,512]{1,0:T(8,128)S(1)} all-gather(f32[49,128]{1,0:T(8,128)S(1)} %pad_maximum_fusion.11), channel_id=1, replica_groups=mesh['groups'=2,'gx'=4,'gy'=4] {'gx'}, dimensions={1}, use_global_device_ids=true | all-gather | bytes 125440 | tf_op jit(solution)/shard_map/all_gather | solution.py:81
  43.9 0.8 copy.172
  44.8 0.7 pad_clamp_fusion
  45.4 1.6 %gather_fusion = f32[128,49]{1,0:T(8,128)S(1)} fusion(f32[49,512]{0,1:T(8,128)} %copy.172, s32[1024]{0:T(1024)S(1)} %pad_clamp_fusion), kind=kCustom, calls=%fused_computation | custom fusion | bytes 50688 | tf_op jit(solution)/shard_map/jit(_take)/gather | solution.py:82
  47.0 0.7 copy.173
  47.7 2.0 %fusion.12 = f32[15,64,128]{2,1,0:T(8,128)} fusion(f32[16,64,128]{2,1,0:T(8,128)} %fusion.11), kind=kLoop, calls=%fused_computation.45 | loop fusion | flops 245760 | bytes 1474560 | tf_op jit(solution)/shard_map/mul | solution.py:145
  49.8 0.8 convert_multiply_fusion
  50.6 1.4 %select_bitcast_fusion = f32[49,128]{1,0:T(8,128)} fusion(f32[128,49]{0,1:T(8,128)} %copy.173, pred[128]{0:T(512)(128)(4,1)} %compare_and_fusion), kind=kLoop, calls=%fused_computation.68 | loop fusion | flops 6272 | bytes 50304 | tf_op jit(solution)/shard_map/jit(_take)/select_n | solution.py:82
  51.9 0.7 fusion.22
  52.6 2.1 %fusion.7 = f32[2,15,64,128]{3,2,1,0:T(8,128)} fusion(f32[1,16,64,128]{3,2,1,0:T(8,128)S(1)} %bitcast.78, f32[1,16,64,128]{3,2,1,0:T(8,128)S(1)} %bitcast.76, f32[15,64,128]{2,1,0:T(8,128)} %fusion.12), kind=kLoop, calls=%fused_computation.26 | loop fusion | flops 983040 | bytes 2523136 | tf_op jit(solution)/shard_map/mul | solution.py:145
  54.7 0.7 fusion.19
  55.4 30.3 %all-reduce.2 = (f32[]{:T(128)}, f32[]{:T(128)}, f32[]{:T(128)}, f32[]{:T(128)}) all-reduce(f32[]{:T(128)} %get-tuple-element.3, f32[]{:T(128)} %get-tuple-element.4, f32[]{:T(128)} %get-tuple-element.5, f32[]{:T(128)} %get-tuple-element.2), channel_id=1, replica_groups=mesh['groups'=2,'gx'=4,'gy'=4] {'gx','gy'}, use_global_device_ids=true, to_apply=%region_5.0 | all-reduce | flops 4 | bytes 32 | tf_op jit(solution)/shard_map/psum | solution.py:59
  88.9 3.0 %copy.162 = f32[65,64,1]{2,0,1:T(8,128)} copy(f32[65,64,1]{0,1,2:T(8,128)} %collective-permute-done) | data formatting | bytes 33280 | tf_op jit(solution)/shard_map/ppermute | solution.py:20
  91.9 3.0 %copy.163 = f32[65,64,1]{2,0,1:T(8,128)} copy(f32[65,64,1]{0,1,2:T(8,128)} %collective-permute-done.1) | data formatting | bytes 33280 | tf_op jit(solution)/shard_map/ppermute | solution.py:22
  94.9 1.5 %pad_maximum_fusion.8 = f32[1,64,130]{2,0,1:T(1,128)S(1)} fusion(f32[65,64,1]{2,0,1:T(8,128)} %copy.163, f32[65,64,128]{2,0,1:T(8,128)S(1)} %dynamic-update-slice.4, f32[65,64,1]{2,0,1:T(8,128)} %copy.162), kind=kLoop, calls=%fused_computation.48 | loop fusion | flops 16640 | bytes 2196480 | tf_op jit(solution)/shard_map/slice | solution.py:101
  96.4 0.4 copy-done
  96.8 0.7 copy-done.1
  97.5 0.9 pad_maximum_fusion
  99.2 1.2 %copy.167 = f32[32,64,130]{2,1,0:T(8,128)S(1)} copy(f32[32,64,130]{2,0,1:T(8,128)S(1)} %pad_maximum_fusion) | data formatting | bytes 2129920 | tf_op jit(solution)/shard_map/slice | solution.py:40
  100.5 0.6 copy.169
  101.1 0.6 copy.166
  101.8 1.1 subtract_multiply_fusion
  102.9 0.7 slice_bitcast_fusion.4
  103.6 0.7 slice_bitcast_fusion.8
  104.3 0.7 pad_maximum_fusion.10
  105.3 0.8 broadcast_maximum_fusion.1
  106.6 0.9 pad_maximum_fusion.4
  107.6 0.7 subtract_multiply_fusion.1
  109.0 0.7 fusion
  109.7 0.8 slice_bitcast_fusion
  110.6 0.8 pad_maximum_fusion.7
  (61 shorter events, 3.3 us)
Async XLA Ops:
  0.6 2.3 %copy-start.8 = (f32[2,16,64,128]{3,2,1,0:T(8,128)S(1)}, f32[2,16,64,128]{3,2,1,0:T(8,128)}, u32[]{:S(2)}) copy-start(f32[2,16,64,128]{3,2,1,0:T(8,128)} %param.10) | copy-start | bytes 3145732
  0.6 2.4 %copy-start.2 = (f32[16,64,128]{2,1,0:T(8,128)S(1)}, f32[16,64,128]{2,1,0:T(8,128)}, u32[]{:S(2)}) copy-start(f32[16,64,128]{2,1,0:T(8,128)} %param.9) | copy-start | bytes 1572868
  3.0 1.8 %copy-start.5 = (f32[1,16,64,128]{3,2,1,0:T(8,128)}, f32[1,16,64,128]{3,2,1,0:T(8,128)S(1)}, u32[]{:S(2)}) copy-start(f32[1,16,64,128]{3,2,1,0:T(8,128)S(1)} %get-tuple-element.19) | copy-start | bytes 1572868
  3.0 1.8 %copy-start.11 = (s32[64,128]{1,0:T(8,128)S(1)}, s32[64,128]{1,0:T(8,128)}, u32[]{:S(2)}) copy-start(s32[64,128]{1,0:T(8,128)} %param.11) | copy-start | bytes 98308
  3.0 1.8 %copy-start.13 = (s32[64,128]{1,0:T(8,128)S(1)}, s32[64,128]{1,0:T(8,128)}, u32[]{:S(2)}) copy-start(s32[64,128]{1,0:T(8,128)} %param.12) | copy-start | bytes 98308
  11.0 15.1 %copy-start.14 = (s32[128]{0:T(128)S(1)}, s32[128]{0:T(128)}, u32[]{:S(2)}) copy-start(s32[128]{0:T(128)} %param.15) | copy-start | bytes 1540
  11.0 16.3 %copy-start.3 = (f32[16,64,128]{2,1,0:T(8,128)S(1)}, f32[16,64,128]{2,1,0:T(8,128)}, u32[]{:S(2)}) copy-start(f32[16,64,128]{2,1,0:T(8,128)} %param.8) | copy-start | bytes 1572868
  11.0 77.9 %collective-permute-start = (f32[65,64,1]{0,1,2:T(8,128)}, f32[65,64,1]{0,1,2:T(8,128)}, u32[]{:S(2)}, u32[]{:S(2)}) collective-permute-start(f32[65,64,1]{0,1,2:T(8,128)} %copy.160), channel_id=1, source_target_pairs={{0,4},{4,8},{8,12},{12,0},{1,5},{5,9},{9,13},{13,1},{2,6},{6,10},{... | collective-permute-start | bytes 49928 | tf_op jit(solution)/shard_map/ppermute | solution.py:20
  17.1 74.8 %collective-permute-start.1 = (f32[65,64,1]{0,1,2:T(8,128)}, f32[65,64,1]{0,1,2:T(8,128)}, u32[]{:S(2)}, u32[]{:S(2)}) collective-permute-start(f32[65,64,1]{0,1,2:T(8,128)} %copy.161), channel_id=1, source_target_pairs={{4,0},{8,4},{12,8},{0,12},{5,1},{9,5},{13,9},{1,13},{6,2},{10,6},{... | collective-permute-start | bytes 49928 | tf_op jit(solution)/shard_map/ppermute | solution.py:22
  19.8 83.1 %collective-permute-start.2 = (f32[65,1,128]{2,0,1:T(8,128)}, f32[65,1,128]{2,0,1:T(8,128)}, u32[]{:S(2)}, u32[]{:S(2)}) collective-permute-start(f32[65,1,128]{2,0,1:T(8,128)} %get-tuple-element.17), channel_id=1, source_target_pairs={{1,0},{2,1},{3,2},{5,4},{6,5},{7,6},{9,8},{10,9},{11,10},{13,12},{... | collective-permute-start | bytes 99848 | tf_op jit(solution)/shard_map/ppermute | solution.py:22
  21.1 83.2 %collective-permute-start.3 = (f32[65,1,128]{2,0,1:T(8,128)}, f32[65,1,128]{2,0,1:T(8,128)}, u32[]{:S(2)}, u32[]{:S(2)}) collective-permute-start(f32[65,1,128]{2,0,1:T(8,128)} %get-tuple-element.16), channel_id=1, source_target_pairs={{0,1},{1,2},{2,3},{4,5},{5,6},{6,7},{8,9},{9,10},{10,11},{12,13},{... | collective-permute-start | bytes 99848 | tf_op jit(solution)/shard_map/ppermute | solution.py:20
  26.1 3.8 %copy-start.9 = (f32[1,16,64,128]{3,1,2,0:T(8,128)}, f32[1,16,64,128]{3,1,2,0:T(8,128)S(1)}, u32[]{:S(2)}) copy-start(f32[1,16,64,128]{3,1,2,0:T(8,128)S(1)} %copy.203) | copy-start | bytes 1572868
  47.7 7.0 %copy-start.10 = (f32[64,128]{1,0:T(8,128)S(1)}, f32[64,128]{1,0:T(8,128)}, u32[]{:S(2)}) copy-start(f32[64,128]{1,0:T(8,128)} %param.14) | copy-start | bytes 98308
  94.9 1.8 %copy-start = (f32[65,64,1]{2,0,1:T(8,128)S(1)}, f32[65,64,1]{2,0,1:T(8,128)}, u32[]{:S(2)}) copy-start(f32[65,64,1]{2,0,1:T(8,128)} %copy.162) | copy-start | bytes 49924
  94.9 2.5 %copy-start.1 = (f32[65,64,1]{2,0,1:T(8,128)S(1)}, f32[65,64,1]{2,0,1:T(8,128)}, u32[]{:S(2)}) copy-start(f32[65,64,1]{2,0,1:T(8,128)} %copy.163) | copy-start | bytes 49924
  101.8 2.5 %slice-start = ((f32[49,128]{1,0:T(8,128)}), f32[32,128]{1,0:T(8,128)S(1)}, s32[]{:S(2)}) async-start(f32[49,128]{1,0:T(8,128)} %select_bitcast_fusion), calls=%async_computation | async-start | bytes 32768 | tf_op jit(solution)/shard_map/slice | solution.py:84
  101.8 2.5 %slice-start.1 = ((f32[49,128]{1,0:T(8,128)}), f32[1,128]{1,0:T(1,128)S(1)}, s32[]{:S(2)}) async-start(f32[49,128]{1,0:T(8,128)} %select_bitcast_fusion), calls=%async_computation.1 | async-start | bytes 1024 | tf_op jit(solution)/shard_map/slice | solution.py:84
  104.3 1.1 copy-start.12
  106.4 1.2 %copy-start.6 = (f32[32,64,128]{2,1,0:T(8,128)S(1)}, f32[32,64,128]{2,1,0:T(8,128)}, u32[]{:S(2)}) copy-start(f32[32,64,128]{2,1,0:T(8,128)} %pad_maximum_fusion.6) | copy-start | bytes 3145732
  106.4 1.2 %slice-start.2 = ((f32[33,128]{1,0:T(8,128)}), f32[32,128]{1,0:T(8,128)S(1)}, s32[]{:S(2)}) async-start(f32[33,128]{1,0:T(8,128)} %copy-done.12), calls=%async_computation.2 | async-start | bytes 32768 | tf_op jit(solution)/shard_map/slice | solution.py:114
  107.6 1.0 copy-start.4
  107.6 1.4 %copy-start.7 = (f32[2,15,64,128]{3,2,1,0:T(8,128)S(1)}, f32[2,15,64,128]{3,2,1,0:T(8,128)}, u32[]{:S(2)}) copy-start(f32[2,15,64,128]{3,2,1,0:T(8,128)} %fusion.7) | copy-start | bytes 2949124
where the time goes:
time: 112 us; the launch traced here: 111 us
  blocking collectives  43.6 us (39%)
  local copies, waits for them, and re-layouts  32.9 us (29%)
  other arithmetic  20.6 us (18%)
  starting transfers between devices  10.1 us (9%)
  between operations  4.18 us (4%)
    psum x1, blocking collectives, shards(): lax.psum((jnp.sum(wet_area), jnp.sum(wet_area * rainfall_input), jnp.sum(...  30.3 us
    all_gather x1, blocking collectives, shards(): gathered = lax.all_gather(top_row, 'gx', axis=1, tiled=True)  13.3 us
    unnamed x37, local copies, waits for them, and re-layouts  7.21 us
    ppermute x2, starting transfers between devices, with_halo(): lax.ppermute(tail, axis, [(i, (i + 1) % count) for i in range(ends)])  6.7 us
    slice x3, local copies, waits for them, and re-layouts, with_halo(): lax.slice_in_dim(cells, cells.shape[dim] - width, cells.shape[dim], axis=...  6.57 us
    mul x2, other arithmetic, shards(): wet_cells[:-1] * wet_cells[1:] * vertical_mixing  4.14 us
    ppermute x2, starting transfers between devices, with_halo(): lax.ppermute(head, axis, [((i + 1) % count, i) for i in range(ends)])  3.37 us
    slice x1, local copies, waits for them, and re-layouts, with_halo(): head = lax.slice_in_dim(cells, 0, width, axis=dim)  3.07 us
  transfers between devices with their start and end apart: 4, of which 0 were waited for; matrix products, arithmetic and copies ran while one was open for 32% of the time, Pallas kernels for 0%

commit v1 on v0

v1 whole, which is shorter than its diff:
```python
import functools

import jax
import jax.numpy as jnp
from jax import lax
from jax.experimental import pallas as pl
from jax.experimental.pallas import tpu as pltpu
from jax.sharding import PartitionSpec as P

time_step = 0.25
diffusivity = 0.5
vertical_mixing = 0.3
top_thickness = 0.5

MESH = pl.DeviceIdType.MESH


def repeat(count, body):
    if count <= 16:
        for i in range(count):
            body(i)
    else:
        pl.loop(0, count)(body)


def face_weights(speed, open_face):
    near_weight = jnp.where(open_face, jnp.maximum(speed, 0.0) + diffusivity, 0.0)
    far_weight = jnp.where(open_face, jnp.minimum(speed, 0.0) - diffusivity, 0.0)
    return near_weight, far_weight


def kernel(
    nx, ny, nk, h, w,
    t_hbm, s_hbm, uv_hbm, sea_hbm, lay_hbm, area_hbm, rain_hbm, seam_smem,
    t_out, s_out,
    t_v, s_v, uv_v, sea_v, lay_v, area_v, rain_v, s0_v, g_v, depth_v,
    pack_v, east_v, west_v, up_v, down_v, south_v, north_v, fold_v, part_v, parts_v,
    load_sems, pack_send, pack_recv, row_send, row_recv, fold_send, fold_recv,
    part_send, part_recv,
):
    mx, my = lax.axis_index("gx"), lax.axis_index("gy")
    is_top = my == ny - 1
    peers = nx * ny - 1

    def peer(r):
        r = r + 1
        return {"gx": lax.rem(mx + r // ny, nx), "gy": lax.rem(my + r % ny, ny)}

    barrier = pltpu.get_barrier_semaphore()

    def greet(r):
        pl.semaphore_signal(barrier, inc=1, device_id=peer(r), device_id_type=MESH)

    repeat(peers, greet)

    loads = [
        pltpu.make_async_copy(src, dst, load_sems.at[i])
        for i, (src, dst) in enumerate(
            [
                (area_hbm, area_v),
                (sea_hbm, sea_v),
                (rain_hbm, rain_v),
                (s_hbm.at[pl.ds(0, h)], s0_v),
                (lay_hbm, lay_v),
                (t_hbm, t_v),
                (s_hbm, s_v),
                (uv_hbm.at[pl.ds(0, nk * h)], uv_v.at[pl.ds(0, nk * h)]),
                (uv_hbm.at[pl.ds(nk * h, nk * h)], uv_v.at[pl.ds(nk * h, nk * h)]),
            ]
        )
    ]
    for load in loads:
        load.start()

    for load in loads[:4]:
        load.wait()
    area = area_v[...]
    sea = sea_v[...]
    wet_area = area * sea.astype(jnp.float32)
    surface = s0_v[...]
    fresh = wet_area * rain_v[...]
    row8 = lax.broadcasted_iota(jnp.int32, (8, w), 0)
    part = jnp.zeros((8, w), jnp.float32)
    for i, term in enumerate((wet_area, fresh, fresh * surface, wet_area * surface)):
        part = jnp.where(row8 == i, jnp.sum(term, axis=0, keepdims=True), part)
    part_v[...] = part
    gain = time_step / area
    g_v[...] = gain

    for load in loads[4:]:
        load.wait()
    depth = (sea * lay_v[...]).astype(jnp.float32)
    depth_v[...] = depth

    lane = lax.broadcasted_iota(jnp.int32, (h, w), 1)
    pair = lane // 2
    packed = jnp.zeros((h, w), jnp.float32)
    for i, ref in enumerate((t_v, s_v, uv_v)):
        for k in range(nk):
            j = i * nk + k
            packed = jnp.where(pair == j, pltpu.roll(ref[pl.ds(k * h, h), :], 2 * j + 1, 1), packed)
    depth_at = 6 * nk
    packed = jnp.where(pair == 3 * nk, pltpu.roll(depth, depth_at + 1, 1), packed)
    pack_v[...] = packed

    def rows(ref, row, base=0):
        return ref[pl.ds(base + row, nk, stride=h), :]

    up_v[pl.ds(0, nk), :] = rows(t_v, h - 1)
    up_v[pl.ds(nk, nk), :] = rows(s_v, h - 1)
    up_v[pl.ds(2 * nk, nk), :] = rows(uv_v, h - 1, nk * h)
    up_v[pl.ds(3 * nk, 8), :] = jnp.broadcast_to(depth[h - 1 : h, :], (8, w))
    down_v[pl.ds(0, nk), :] = rows(t_v, 0)
    down_v[pl.ds(nk, nk), :] = rows(s_v, 0)
    down_v[pl.ds(2 * nk, 8), :] = jnp.broadcast_to(depth[0:1, :], (8, w))

    @pl.when(is_top)
    def _():
        up = up_v[...]
        flip = (w - 1) - lax.broadcasted_iota(jnp.int32, up.shape, 1)
        fold_v[mx] = jnp.take_along_axis(up, flip, axis=1)

    pl.semaphore_wait(barrier, peers)

    def part_copy(r):
        return pltpu.make_async_remote_copy(
            src_ref=part_v, dst_ref=parts_v.at[r],
            send_sem=part_send.at[r], recv_sem=part_recv.at[r],
            device_id=peer(r), device_id_type=MESH,
        )

    repeat(peers, lambda r: part_copy(r).start())

    to_east = pltpu.make_async_remote_copy(
        src_ref=pack_v, dst_ref=west_v, send_sem=pack_send.at[0], recv_sem=pack_recv.at[0],
        device_id={"gx": lax.rem(mx + 1, nx)}, device_id_type=MESH,
    )
    to_west = pltpu.make_async_remote_copy(
        src_ref=pack_v, dst_ref=east_v, send_sem=pack_send.at[1], recv_sem=pack_recv.at[1],
        device_id={"gx": lax.rem(mx + nx - 1, nx)}, device_id_type=MESH,
    )
    to_north = pltpu.make_async_remote_copy(
        src_ref=up_v, dst_ref=south_v, send_sem=row_send.at[0], recv_sem=row_recv.at[0],
        device_id={"gy": lax.rem(my + 1, ny)}, device_id_type=MESH,
    )
    to_south = pltpu.make_async_remote_copy(
        src_ref=down_v, dst_ref=north_v, send_sem=row_send.at[1], recv_sem=row_recv.at[1],
        device_id={"gy": lax.rem(my + ny - 1, ny)}, device_id_type=MESH,
    )

    def fold_copy(d):
        return pltpu.make_async_remote_copy(
            src_ref=fold_v.at[mx], dst_ref=fold_v.at[mx],
            send_sem=fold_send.at[d], recv_sem=fold_recv.at[d],
            device_id={"gx": lax.rem(mx + d + 1, nx)}, device_id_type=MESH,
        )

    to_east.start()
    to_west.start()

    @pl.when(jnp.logical_not(is_top))
    def _():
        to_north.start()

    @pl.when(my > 0)
    def _():
        to_south.start()

    @pl.when(is_top)
    def _():
        repeat(nx - 1, lambda d: fold_copy(d).start())

    row = lax.broadcasted_iota(jnp.int32, (h, w), 0)
    depth_east = jnp.where(lane == w - 1, 0.0, jnp.minimum(depth, pltpu.roll(depth, w - 1, 1)))
    depth_north = jnp.where(row == h - 1, 0.0, jnp.minimum(depth, pltpu.roll(depth, h - 1, 0)))

    def level(k, above):
        kf = k.astype(jnp.float32)
        at = pl.ds(pl.multiple_of(k * h, h), h)
        below = pl.ds(pl.multiple_of(jnp.minimum(k + 1, nk - 1) * h, h), h)
        east_near, east_far = face_weights(uv_v[at, :], depth_east > kf)
        north_near, north_far = face_weights(
            uv_v[pl.ds(pl.multiple_of((k + nk) * h, h), h), :], depth_north > kf
        )
        mix = jnp.where(depth_v[...] > kf + 1.0, time_step * vertical_mixing, 0.0)
        gain = g_v[...]
        falls = []
        for ref, out, came in ((t_v, t_out, above[0]), (s_v, s_out, above[1])):
            c = ref[at, :]
            east = east_near * c + east_far * pltpu.roll(c, w - 1, 1)
            north = north_near * c + north_far * pltpu.roll(c, h - 1, 0)
            flow = (pltpu.roll(east, 1, 1) - east) + (pltpu.roll(north, 1, 0) - north)
            fall = mix * (c - ref[below, :])
            out[at, :] = c + (gain * flow + (came - fall))
            falls.append(fall)
        return tuple(falls)

    zero = jnp.zeros((h, w), jnp.float32)
    lax.fori_loop(0, nk, level, (zero, zero))

    to_east.wait()
    to_west.wait()
    mine, east_side, west_side = pack_v[...], east_v[...], west_v[...]
    even = lane % 2 == 0

    def speeds(cells):
        return jnp.where(
            pair < nk, pltpu.roll(cells, w - 4 * nk, 1), pltpu.roll(cells, w - 2 * nk, 1)
        )

    def column(cells, at):
        return jnp.broadcast_to(cells[:, at : at + 1], (h, w))

    near = jnp.where(even, mine, pltpu.roll(west_side, 1, 1))
    far = jnp.where(even, pltpu.roll(east_side, w - 1, 1), mine)
    speed = jnp.where(even, speeds(mine), pltpu.roll(speeds(west_side), 1, 1))
    shallow = jnp.where(
        even,
        jnp.minimum(column(mine, depth_at), column(east_side, depth_at + 1)),
        jnp.minimum(column(mine, depth_at + 1), column(west_side, depth_at)),
    )
    near_weight, far_weight = face_weights(speed, shallow > (pair % nk).astype(jnp.float32))
    gain = g_v[...]
    edge_gain = jnp.where(even, -column(gain, w - 1), column(gain, 0))
    edge = edge_gain * (near_weight * near + far_weight * far)
    at_edge = (lane == 0) | (lane == w - 1)
    for i, out in enumerate((t_out, s_out)):
        for k in range(nk):
            shift = (w - (2 * (i * nk + k) + 1)) % w
            out[pl.ds(k * h, h), :] += jnp.where(at_edge, pltpu.roll(edge, shift, 1), 0.0)

    level_row = lax.broadcasted_iota(jnp.int32, (nk, w), 0).astype(jnp.float32)

    def north_edge(far_t, far_s, speed, far_depth):
        near_weight, far_weight = face_weights(
            speed, jnp.minimum(up_v[3 * nk : 3 * nk + 1, :], far_depth) > level_row
        )
        for near, far, out in (
            (up_v[pl.ds(0, nk), :], far_t, t_out),
            (up_v[pl.ds(nk, nk), :], far_s, s_out),
        ):
            at = pl.ds(h - 1, nk, stride=h)
            out[at, :] -= g_v[h - 1 : h, :] * (near_weight * near + far_weight * far)

    @pl.when(is_top)
    def _():
        repeat(nx - 1, lambda d: fold_copy(d).wait())
        partner = fold_v[seam_smem[0] // w]
        north_edge(
            partner[:nk],
            partner[nk : 2 * nk],
            0.5 * (up_v[pl.ds(2 * nk, nk), :] - partner[2 * nk : 3 * nk]),
            partner[3 * nk : 3 * nk + 1],
        )

    @pl.when(jnp.logical_not(is_top))
    def _():
        to_north.wait_send()
        to_south.wait_recv()
        north_edge(
            north_v[pl.ds(0, nk), :],
            north_v[pl.ds(nk, nk), :],
            up_v[pl.ds(2 * nk, nk), :],
            north_v[2 * nk : 2 * nk + 1, :],
        )

    @pl.when(my > 0)
    def _():
        to_south.wait_send()
        to_north.wait_recv()
        near_weight, far_weight = face_weights(
            south_v[pl.ds(2 * nk, nk), :],
            jnp.minimum(down_v[2 * nk : 2 * nk + 1, :], south_v[3 * nk : 3 * nk + 1, :]) > level_row,
        )
        for i, out in enumerate((t_out, s_out)):
            at = pl.ds(0, nk, stride=h)
            out[at, :] += g_v[0:1, :] * (
                near_weight * south_v[pl.ds(i * nk, nk), :]
                + far_weight * down_v[pl.ds(i * nk, nk), :]
            )

    repeat(peers, lambda r: part_copy(r).wait())
    totals = part_v[...] + jnp.sum(parts_v[...], axis=0)
    totals = jnp.sum(totals, axis=1, keepdims=True)
    total_area, total_fresh = totals[0:1], totals[1:2]
    salt_fresh, salt_only = totals[2:3], totals[3:4]
    mean_fresh = total_fresh / total_area
    lift = (salt_fresh - mean_fresh * salt_only) / total_area
    virtual = lift - s0_v[...] * (rain_v[...] - mean_fresh)
    s_out[pl.ds(0, h), :] += jnp.where(depth_v[...] > 0.0, time_step / top_thickness * virtual, 0.0)


def shards(nx, ny, t, s, uv, sea, layers, area, rain, seam):
    nk, h, w = t.shape
    assert w == 128 and h % 8 == 0 and nk % 8 == 0 and 6 * nk + 2 <= w
    f32 = jnp.float32
    peers = nx * ny - 1
    any_space = pl.BlockSpec(memory_space=pl.ANY)
    dma = pltpu.SemaphoreType.DMA
    plane = pltpu.VMEM((h, w), f32)
    t_next, s_next = pl.pallas_call(
        functools.partial(kernel, nx, ny, nk, h, w),
        out_shape=[jax.ShapeDtypeStruct((nk * h, w), f32)] * 2,
        in_specs=[any_space] * 7 + [pl.BlockSpec(memory_space=pltpu.SMEM)],
        out_specs=[pl.BlockSpec(memory_space=pltpu.VMEM)] * 2,
        scratch_shapes=[
            pltpu.VMEM((nk * h, w), f32),
            pltpu.VMEM((nk * h, w), f32),
            pltpu.VMEM((2 * nk * h, w), f32),
            pltpu.VMEM((h, w), jnp.int32),
            pltpu.VMEM((h, w), jnp.int32),
            plane, plane, plane, plane, plane,
            plane, plane, plane,
            pltpu.VMEM((3 * nk + 8, w), f32),
            pltpu.VMEM((2 * nk + 8, w), f32),
            pltpu.VMEM((3 * nk + 8, w), f32),
            pltpu.VMEM((2 * nk + 8, w), f32),
            pltpu.VMEM((nx, 3 * nk + 8, w), f32),
            pltpu.VMEM((8, w), f32),
            pltpu.VMEM((peers, 8, w), f32),
            dma((9,)), dma((2,)), dma((2,)), dma((2,)), dma((2,)),
            dma((nx - 1,)), dma((nx - 1,)), dma((peers,)), dma((peers,)),
        ],
        compiler_params=pltpu.CompilerParams(collective_id=0, has_side_effects=True),
        name="tracer_step",
    )(
        t.reshape(nk * h, w), s.reshape(nk * h, w), uv.reshape(2 * nk * h, w),
        sea, layers, area, rain, seam,
    )
    return t_next.reshape(t.shape), s_next.reshape(s.shape)


def solution(mesh):
    in_specs = (
        P("groups", "gy", "gx"),
        P("groups", "gy", "gx"),
        P("groups", None, "gy", "gx"),
        P("gy", "gx"),
        P("gy", "gx"),
        P("gy", "gx"),
        P("gy", "gx"),
        P("gx"),
    )
    out_specs = (P("groups", "gy", "gx"), P("groups", "gy", "gx"))
    return jax.shard_map(
        functools.partial(shards, mesh.shape["gx"], mesh.shape["gy"]),
        mesh=mesh, in_specs=in_specs, out_specs=out_specs, check_vma=False,
    )
```

time: 112 us -> 16.5 us (0.15)
  blocking collectives: 43.6 us -> 0 us
  local copies, waits for them, and re-layouts: 32.9 us -> 2.74 us
  other arithmetic: 20.6 us -> 0 us
  Pallas kernels: 0 us -> 12.9 us
  starting transfers between devices: 10.1 us -> 0 us
  between operations: 4.18 us -> 0.65 us
    psum x1 -> x0, blocking collectives: 30.3 us -> none  [shards(): lax.psum((jnp.sum(wet_area), jnp.sum(wet_area * rainfall_input), jnp.sum(...]
    all_gather x1 -> x0, blocking collectives: 13.3 us -> none  [shards(): gathered = lax.all_gather(top_row, 'gx', axis=1, tiled=True)]
    pallas_call x0 -> x1, Pallas kernels: none -> 12.9 us  [shards(): pl.pallas_call(functools.partial(kernel, nx, ny, nk, h, w), out_shape=[ja...]
    slice x14 -> x0, local copies, waits for them, and re-layouts: 11 us -> none  [the longest x3 6.57 us: with_halo(): lax.slice_in_dim(cells, cells.shape[dim] - width, cells.shape[dim], axis=...]
    ppermute x4 -> x0, starting transfers between devices: 10.1 us -> none  [the longest x2 6.7 us: with_halo(): lax.ppermute(tail, axis, [(i, (i + 1) % count) for i in range(ends)])]
    mul x7 -> x0, other arithmetic: 7.14 us -> none  [the longest x2 4.14 us: shards(): wet_cells[:-1] * wet_cells[1:] * vertical_mixing]
    ppermute x2 -> x0, local copies, waits for them, and re-layouts: 6.03 us -> none  [the longest x1 3.02 us: with_halo(): lax.ppermute(tail, axis, [(i, (i + 1) % count) for i in range(ends)])]
    concatenate x7 -> x0, other arithmetic: 4.47 us -> none  [the longest x2 1.83 us: with_halo(): jnp.concatenate([lax.ppermute(tail, axis, [(i, (i + 1) % count) for i in...]
  transfers between devices with their start and end apart: 4 -> 0, of which waited for: 0 -> 0; matrix products, arithmetic and copies ran while one was open for 32% -> 0% of each run, Pallas kernels for 0% -> 0%
where the time goes in v1:
time: 16.5 us; the launch traced here: 16.3 us
  Pallas kernels  12.9 us (78%)
  local copies, waits for them, and re-layouts  2.74 us (17%)
  between operations  0.65 us (4%)
    pallas_call x1, Pallas kernels, shards(): pl.pallas_call(functools.partial(kernel, nx, ny, nk, h, w), out_shape=[ja...  12.9 us
    unnamed x4, local copies, waits for them, and re-layouts  2.74 us

profile of v1, /device:TPU:0, one launch (start us, length us, event | category | flops | bytes accessed | tf_op | source)
XLA Modules:
  0.0 16.3 jit_solution(3051631202088292288)
XLA Ops:
  0.6 12.9 %tracer_step.1 = (f32[1024,128]{1,0:T(8,128)}, f32[1024,128]{1,0:T(8,128)}) custom-call(f32[1024,128]{1,0:T(8,128)} %bitcast.6, f32[1024,128]{1,0:T(8,128)} %bitcast.7, f32[2048,128]{1,0:T(8,128)} %bitcast.5, s32[64,128]{1,0:T(8,128)} %sea_hbm.1, s32[64,128]{1,0:T(8,128)} %lay_hbm.1, f32[64,128]{1,0:T(8,128)} %area_hbm.1, f32[64,128]{1,0:T(8,128)} %rain_hbm.1, ...), custom_call_target="tpu_custom_call" | custom-call | tf_op jit(solution)/shard_map/tracer_step/pallas_call | solution.py:301
  13.6 0.0 copy-start
  13.6 1.9 %copy.12 = f32[16,64,128]{2,1,0:T(8,128)} copy(f32[16,64,128]{2,1,0:T(8,128)} %bitcast.9) | data formatting | bytes 1048576
  15.5 0.0 copy-done
  15.5 0.8 %copy.13 = f32[16,64,128]{2,1,0:T(8,128)} copy(f32[16,64,128]{2,1,0:T(8,128)S(1)} %bitcast.8) | data formatting | bytes 1048576
Async XLA Ops:
  13.6 2.0 %copy-start = (f32[1024,128]{1,0:T(8,128)S(1)}, f32[1024,128]{1,0:T(8,128)}, u32[]{:S(2)}) copy-start(f32[1024,128]{1,0:T(8,128)} %get-tuple-element.5) | copy-start | bytes 1572868

commit v2 on v1

--- a/solution.py
+++ b/solution.py
@@ -290,6 +290,24 @@
     s_out[pl.ds(0, h), :] += jnp.where(depth_v[...] > 0.0, time_step / top_thickness * virtual, 0.0)
 
 
+store_cuts = 4
+
+
+def store_kernel(t_ref, s_ref, t_out, s_out, sems):
+    step = t_ref.shape[0] // store_cuts
+    copies = [
+        pltpu.make_async_copy(
+            src.at[pl.ds(i * step, step)], dst.at[pl.ds(i * step, step)], sems.at[2 * i + n]
+        )
+        for i in range(store_cuts)
+        for n, (src, dst) in enumerate(((t_ref, t_out), (s_ref, s_out)))
+    ]
+    for copy in copies:
+        copy.start()
+    for copy in copies:
+        copy.wait()
+
+
 def shards(nx, ny, t, s, uv, sea, layers, area, rain, seam):
     nk, h, w = t.shape
     assert w == 128 and h % 8 == 0 and nk % 8 == 0 and 6 * nk + 2 <= w
@@ -300,7 +318,7 @@
     plane = pltpu.VMEM((h, w), f32)
     t_next, s_next = pl.pallas_call(
         functools.partial(kernel, nx, ny, nk, h, w),
-        out_shape=[jax.ShapeDtypeStruct((nk * h, w), f32)] * 2,
+        out_shape=[pltpu.VMEM((nk * h, w), f32)] * 2,
         in_specs=[any_space] * 7 + [pl.BlockSpec(memory_space=pltpu.SMEM)],
         out_specs=[pl.BlockSpec(memory_space=pltpu.VMEM)] * 2,
         scratch_shapes=[
@@ -321,12 +339,23 @@
             dma((9,)), dma((2,)), dma((2,)), dma((2,)), dma((2,)),
             dma((nx - 1,)), dma((nx - 1,)), dma((peers,)), dma((peers,)),
         ],
-        compiler_params=pltpu.CompilerParams(collective_id=0, has_side_effects=True),
+        compiler_params=pltpu.CompilerParams(
+            collective_id=0, has_side_effects=True, vmem_limit_bytes=65990000
+        ),
         name="tracer_step",
     )(
         t.reshape(nk * h, w), s.reshape(nk * h, w), uv.reshape(2 * nk * h, w),
         sea, layers, area, rain, seam,
     )
+    t_next, s_next = pl.pallas_call(
+        store_kernel,
+        out_shape=[jax.ShapeDtypeStruct((nk * h, w), f32)] * 2,
+        in_specs=[any_space] * 2,
+        out_specs=[any_space] * 2,
+        scratch_shapes=[dma((2 * store_cuts,))],
+        compiler_params=pltpu.CompilerParams(vmem_limit_bytes=8 << 20),
+        name="store",
+    )(t_next, s_next)
     return t_next.reshape(t.shape), s_next.reshape(s.shape)
 
 

time: 16.5 us -> 13.9 us (0.84)
  local copies, waits for them, and re-layouts: 2.74 us -> 0 us
  Pallas kernels: 12.9 us -> 13.1 us
    unnamed x4 -> x0, local copies, waits for them, and re-layouts: 2.74 us -> none
    pallas_call x1 -> x2, Pallas kernels: 12.9 us -> 13.1 us  [the longest x1 12.1 us: shards(): pl.pallas_call(functools.partial(kernel, nx, ny, nk, h, w), out_shape=[pl...]
where the time goes in v2:
time: 13.9 us; the launch traced here: 13.8 us
  Pallas kernels  13.1 us (94%)
  between operations  0.64 us (5%)
    pallas_call x1, Pallas kernels, shards(): pl.pallas_call(functools.partial(kernel, nx, ny, nk, h, w), out_shape=[pl...  12.1 us
    pallas_call x1, Pallas kernels, shards(): pl.pallas_call(store_kernel, out_shape=[jax.ShapeDtypeStruct((nk * h, w),...  1.03 us

profile of v2, /device:TPU:0, one launch (start us, length us, event | category | flops | bytes accessed | tf_op | source)
XLA Modules:
  0.0 13.8 jit_solution(9725808399673899538)
XLA Ops:
  0.6 12.1 %tracer_step.1 = (f32[1024,128]{1,0:T(8,128)S(1)}, f32[1024,128]{1,0:T(8,128)S(1)}) custom-call(f32[1024,128]{1,0:T(8,128)} %bitcast.6, f32[1024,128]{1,0:T(8,128)} %bitcast.7, f32[2048,128]{1,0:T(8,128)} %bitcast.5, s32[64,128]{1,0:T(8,128)} %sea_hbm.1, s32[64,128]{1,0:T(8,128)} %lay_hbm.1, f32[64,128]{1,0:T(8,128)} %area_hbm.1, f32[64,128]{1,0:T(8,128)} %rain_hbm.1, ...), custom_call_target="tpu_custom_call" | custom-call | tf_op jit(solution)/shard_map/tracer_step/pallas_call | solution.py:319
  12.7 1.0 %store.1 = (f32[1024,128]{1,0:T(8,128)}, f32[1024,128]{1,0:T(8,128)}) custom-call(f32[1024,128]{1,0:T(8,128)S(1)} %get-tuple-element.6.t_ref, f32[1024,128]{1,0:T(8,128)S(1)} %get-tuple-element.7.s_ref), custom_call_target="tpu_custom_call" | custom-call | tf_op jit(solution)/shard_map/store/pallas_call | solution.py:350

commit v3 on v2

--- a/solution.py
+++ b/solution.py
@@ -34,7 +34,8 @@
     t_hbm, s_hbm, uv_hbm, sea_hbm, lay_hbm, area_hbm, rain_hbm, seam_smem,
     t_out, s_out,
     t_v, s_v, uv_v, sea_v, lay_v, area_v, rain_v, s0_v, g_v, depth_v,
-    pack_v, east_v, west_v, up_v, down_v, south_v, north_v, fold_v, part_v, parts_v,
+    pack_v, last_v, first_v, east_v, west_v, up_v, down_v, south_v, north_v, fold_v,
+    part_v, parts_v,
     load_sems, pack_send, pack_recv, row_send, row_recv, fold_send, fold_recv,
     part_send, part_recv,
 ):
@@ -87,6 +88,17 @@
     gain = time_step / area
     g_v[...] = gain
 
+    pl.semaphore_wait(barrier, peers)
+
+    def part_copy(r):
+        return pltpu.make_async_remote_copy(
+            src_ref=part_v, dst_ref=parts_v.at[r],
+            send_sem=part_send.at[r], recv_sem=part_recv.at[r],
+            device_id=peer(r), device_id_type=MESH,
+        )
+
+    repeat(peers, lambda r: part_copy(r).start())
+
     for load in loads[4:]:
         load.wait()
     depth = (sea * lay_v[...]).astype(jnp.float32)
@@ -102,6 +114,21 @@
     depth_at = 6 * nk
     packed = jnp.where(pair == 3 * nk, pltpu.roll(depth, depth_at + 1, 1), packed)
     pack_v[...] = packed
+    half = h // 2
+    even_half = lane[:half] % 2 == 0
+    last_v[...] = jnp.where(even_half, packed[:half], pltpu.roll(packed[half:], 1, 1))
+    first_v[...] = jnp.where(even_half, pltpu.roll(packed[half:], w - 1, 1), packed[:half])
+
+    to_east = pltpu.make_async_remote_copy(
+        src_ref=last_v, dst_ref=west_v, send_sem=pack_send.at[0], recv_sem=pack_recv.at[0],
+        device_id={"gx": lax.rem(mx + 1, nx)}, device_id_type=MESH,
+    )
+    to_west = pltpu.make_async_remote_copy(
+        src_ref=first_v, dst_ref=east_v, send_sem=pack_send.at[1], recv_sem=pack_recv.at[1],
+        device_id={"gx": lax.rem(mx + nx - 1, nx)}, device_id_type=MESH,
+    )
+    to_east.start()
+    to_west.start()
 
     def rows(ref, row, base=0):
         return ref[pl.ds(base + row, nk, stride=h), :]
@@ -120,25 +147,6 @@
         flip = (w - 1) - lax.broadcasted_iota(jnp.int32, up.shape, 1)
         fold_v[mx] = jnp.take_along_axis(up, flip, axis=1)
 
-    pl.semaphore_wait(barrier, peers)
-
-    def part_copy(r):
-        return pltpu.make_async_remote_copy(
-            src_ref=part_v, dst_ref=parts_v.at[r],
-            send_sem=part_send.at[r], recv_sem=part_recv.at[r],
-            device_id=peer(r), device_id_type=MESH,
-        )
-
-    repeat(peers, lambda r: part_copy(r).start())
-
-    to_east = pltpu.make_async_remote_copy(
-        src_ref=pack_v, dst_ref=west_v, send_sem=pack_send.at[0], recv_sem=pack_recv.at[0],
-        device_id={"gx": lax.rem(mx + 1, nx)}, device_id_type=MESH,
-    )
-    to_west = pltpu.make_async_remote_copy(
-        src_ref=pack_v, dst_ref=east_v, send_sem=pack_send.at[1], recv_sem=pack_recv.at[1],
-        device_id={"gx": lax.rem(mx + nx - 1, nx)}, device_id_type=MESH,
-    )
     to_north = pltpu.make_async_remote_copy(
         src_ref=up_v, dst_ref=south_v, send_sem=row_send.at[0], recv_sem=row_recv.at[0],
         device_id={"gy": lax.rem(my + 1, ny)}, device_id_type=MESH,
@@ -155,8 +163,6 @@
             device_id={"gx": lax.rem(mx + d + 1, nx)}, device_id_type=MESH,
         )
 
-    to_east.start()
-    to_west.start()
 
     @pl.when(jnp.logical_not(is_top))
     def _():
@@ -200,7 +206,9 @@
 
     to_east.wait()
     to_west.wait()
-    mine, east_side, west_side = pack_v[...], east_v[...], west_v[...]
+    mine, east_half, west_half = pack_v[...], east_v[...], west_v[...]
+    east_side = jnp.concatenate([east_half, pltpu.roll(east_half, 1, 1)], axis=0)
+    west_side = jnp.concatenate([west_half, pltpu.roll(west_half, w - 1, 1)], axis=0)
     even = lane % 2 == 0
 
     def speeds(cells):
@@ -310,9 +318,10 @@
 
 def shards(nx, ny, t, s, uv, sea, layers, area, rain, seam):
     nk, h, w = t.shape
-    assert w == 128 and h % 8 == 0 and nk % 8 == 0 and 6 * nk + 2 <= w
+    assert w == 128 and h % 16 == 0 and nk % 8 == 0 and 6 * nk + 2 <= w
     f32 = jnp.float32
     peers = nx * ny - 1
+    half_plane = pltpu.VMEM((h // 2, w), f32)
     any_space = pl.BlockSpec(memory_space=pl.ANY)
     dma = pltpu.SemaphoreType.DMA
     plane = pltpu.VMEM((h, w), f32)
@@ -328,7 +337,7 @@
             pltpu.VMEM((h, w), jnp.int32),
             pltpu.VMEM((h, w), jnp.int32),
             plane, plane, plane, plane, plane,
-            plane, plane, plane,
+            plane, half_plane, half_plane, half_plane, half_plane,
             pltpu.VMEM((3 * nk + 8, w), f32),
             pltpu.VMEM((2 * nk + 8, w), f32),
             pltpu.VMEM((3 * nk + 8, w), f32),

time: 13.9 us -> 13.1 us (0.942)
  Pallas kernels: 13.1 us -> 12.3 us
    pallas_call x1, Pallas kernels: 12.1 us -> 11.3 us  [shards(): pl.pallas_call(functools.partial(kernel, nx, ny, nk, h, w), out_shape=[pl...]
where the time goes in v3:
time: 13.1 us; the launch traced here: 12.9 us
  Pallas kernels  12.3 us (94%)
  between operations  0.64 us (5%)
    pallas_call x1, Pallas kernels, shards(): pl.pallas_call(functools.partial(kernel, nx, ny, nk, h, w), out_shape=[pl...  11.3 us
    pallas_call x1, Pallas kernels, shards(): pl.pallas_call(store_kernel, out_shape=[jax.ShapeDtypeStruct((nk * h, w),...  1.03 us

profile of v3, /device:TPU:0, one launch (start us, length us, event | category | flops | bytes accessed | tf_op | source)
XLA Modules:
  0.0 12.9 jit_solution(6924270220141044757)
XLA Ops:
  0.6 11.3 %tracer_step.1 = (f32[1024,128]{1,0:T(8,128)S(1)}, f32[1024,128]{1,0:T(8,128)S(1)}) custom-call(f32[1024,128]{1,0:T(8,128)} %bitcast.6, f32[1024,128]{1,0:T(8,128)} %bitcast.7, f32[2048,128]{1,0:T(8,128)} %bitcast.5, s32[64,128]{1,0:T(8,128)} %sea_hbm.1, s32[64,128]{1,0:T(8,128)} %lay_hbm.1, f32[64,128]{1,0:T(8,128)} %area_hbm.1, f32[64,128]{1,0:T(8,128)} %rain_hbm.1, ...), custom_call_target="tpu_custom_call" | custom-call | tf_op jit(solution)/shard_map/tracer_step/pallas_call | solution.py:328
  11.9 1.0 %store.1 = (f32[1024,128]{1,0:T(8,128)}, f32[1024,128]{1,0:T(8,128)}) custom-call(f32[1024,128]{1,0:T(8,128)S(1)} %get-tuple-element.6.t_ref, f32[1024,128]{1,0:T(8,128)S(1)} %get-tuple-element.7.s_ref), custom_call_target="tpu_custom_call" | custom-call | tf_op jit(solution)/shard_map/store/pallas_call | solution.py:359

commit v4 on v3

--- a/solution.py
+++ b/solution.py
@@ -204,6 +204,45 @@
     zero = jnp.zeros((h, w), jnp.float32)
     lax.fori_loop(0, nk, level, (zero, zero))
 
+    level_row = lax.broadcasted_iota(jnp.int32, (nk, w), 0).astype(jnp.float32)
+
+    def north_edge(far_t, far_s, speed, far_depth):
+        near_weight, far_weight = face_weights(
+            speed, jnp.minimum(up_v[3 * nk : 3 * nk + 1, :], far_depth) > level_row
+        )
+        for near, far, out in (
+            (up_v[pl.ds(0, nk), :], far_t, t_out),
+            (up_v[pl.ds(nk, nk), :], far_s, s_out),
+        ):
+            at = pl.ds(h - 1, nk, stride=h)
+            out[at, :] -= g_v[h - 1 : h, :] * (near_weight * near + far_weight * far)
+
+    @pl.when(jnp.logical_not(is_top))
+    def _():
+        to_north.wait_send()
+        to_south.wait_recv()
+        north_edge(
+            north_v[pl.ds(0, nk), :],
+            north_v[pl.ds(nk, nk), :],
+            up_v[pl.ds(2 * nk, nk), :],
+            north_v[2 * nk : 2 * nk + 1, :],
+        )
+
+    @pl.when(my > 0)
+    def _():
+        to_south.wait_send()
+        to_north.wait_recv()
+        near_weight, far_weight = face_weights(
+            south_v[pl.ds(2 * nk, nk), :],
+            jnp.minimum(down_v[2 * nk : 2 * nk + 1, :], south_v[3 * nk : 3 * nk + 1, :]) > level_row,
+        )
+        for i, out in enumerate((t_out, s_out)):
+            at = pl.ds(0, nk, stride=h)
+            out[at, :] += g_v[0:1, :] * (
+                near_weight * south_v[pl.ds(i * nk, nk), :]
+                + far_weight * down_v[pl.ds(i * nk, nk), :]
+            )
+
     to_east.wait()
     to_west.wait()
     mine, east_half, west_half = pack_v[...], east_v[...], west_v[...]
@@ -237,19 +276,6 @@
             shift = (w - (2 * (i * nk + k) + 1)) % w
             out[pl.ds(k * h, h), :] += jnp.where(at_edge, pltpu.roll(edge, shift, 1), 0.0)
 
-    level_row = lax.broadcasted_iota(jnp.int32, (nk, w), 0).astype(jnp.float32)
-
-    def north_edge(far_t, far_s, speed, far_depth):
-        near_weight, far_weight = face_weights(
-            speed, jnp.minimum(up_v[3 * nk : 3 * nk + 1, :], far_depth) > level_row
-        )
-        for near, far, out in (
-            (up_v[pl.ds(0, nk), :], far_t, t_out),
-            (up_v[pl.ds(nk, nk), :], far_s, s_out),
-        ):
-            at = pl.ds(h - 1, nk, stride=h)
-            out[at, :] -= g_v[h - 1 : h, :] * (near_weight * near + far_weight * far)
-
     @pl.when(is_top)
     def _():
         repeat(nx - 1, lambda d: fold_copy(d).wait())
@@ -260,32 +286,6 @@
             0.5 * (up_v[pl.ds(2 * nk, nk), :] - partner[2 * nk : 3 * nk]),
             partner[3 * nk : 3 * nk + 1],
         )
-
-    @pl.when(jnp.logical_not(is_top))
-    def _():
-        to_north.wait_send()
-        to_south.wait_recv()
-        north_edge(
-            north_v[pl.ds(0, nk), :],
-            north_v[pl.ds(nk, nk), :],
-            up_v[pl.ds(2 * nk, nk), :],
-            north_v[2 * nk : 2 * nk + 1, :],
-        )
-
-    @pl.when(my > 0)
-    def _():
-        to_south.wait_send()
-        to_north.wait_recv()
-        near_weight, far_weight = face_weights(
-            south_v[pl.ds(2 * nk, nk), :],
-            jnp.minimum(down_v[2 * nk : 2 * nk + 1, :], south_v[3 * nk : 3 * nk + 1, :]) > level_row,
-        )
-        for i, out in enumerate((t_out, s_out)):
-            at = pl.ds(0, nk, stride=h)
-            out[at, :] += g_v[0:1, :] * (
-                near_weight * south_v[pl.ds(i * nk, nk), :]
-                + far_weight * down_v[pl.ds(i * nk, nk), :]
-            )
 
     repeat(peers, lambda r: part_copy(r).wait())
     totals = part_v[...] + jnp.sum(parts_v[...], axis=0)
@@ -298,7 +298,7 @@
     s_out[pl.ds(0, h), :] += jnp.where(depth_v[...] > 0.0, time_step / top_thickness * virtual, 0.0)
 
 
-store_cuts = 4
+store_cuts = 1
 
 
 def store_kernel(t_ref, s_ref, t_out, s_out, sems):

time: 13.1 us -> 13 us (level)
  no operation moved by 1% of the time
where the time goes in v4:
time: 13 us; the launch traced here: 12.9 us
  Pallas kernels  12.2 us (94%)
  between operations  0.64 us (5%)
    pallas_call x1, Pallas kernels, shards(): pl.pallas_call(functools.partial(kernel, nx, ny, nk, h, w), out_shape=[pl...  11.3 us
    pallas_call x1, Pallas kernels, shards(): pl.pallas_call(store_kernel, out_shape=[jax.ShapeDtypeStruct((nk * h, w),...  0.99 us

profile of v4, /device:TPU:0, one launch (start us, length us, event | category | flops | bytes accessed | tf_op | source)
XLA Modules:
  0.0 12.9 jit_solution(14339968744811108493)
XLA Ops:
  0.6 11.3 %tracer_step.1 = (f32[1024,128]{1,0:T(8,128)S(1)}, f32[1024,128]{1,0:T(8,128)S(1)}) custom-call(f32[1024,128]{1,0:T(8,128)} %bitcast.6, f32[1024,128]{1,0:T(8,128)} %bitcast.7, f32[2048,128]{1,0:T(8,128)} %bitcast.5, s32[64,128]{1,0:T(8,128)} %sea_hbm.1, s32[64,128]{1,0:T(8,128)} %lay_hbm.1, f32[64,128]{1,0:T(8,128)} %area_hbm.1, f32[64,128]{1,0:T(8,128)} %rain_hbm.1, ...), custom_call_target="tpu_custom_call" | custom-call | tf_op jit(solution)/shard_map/tracer_step/pallas_call | solution.py:328
  11.9 1.0 %store.1 = (f32[1024,128]{1,0:T(8,128)}, f32[1024,128]{1,0:T(8,128)}) custom-call(f32[1024,128]{1,0:T(8,128)S(1)} %get-tuple-element.6.t_ref, f32[1024,128]{1,0:T(8,128)S(1)} %get-tuple-element.7.s_ref), custom_call_target="tpu_custom_call" | custom-call | tf_op jit(solution)/shard_map/store/pallas_call | solution.py:359
